TPU v7x, 32 devices: a whole 2x2x4 slice. The times are simulated.
32 devices in a mesh: prow: 4 (over y, core), pcol: 8 (over z, x).
Axes of the slice: x: 2, y: 2, z: 4, core: 2. Of those that a mesh axis runs over, the one named last changes fastest.
Arguments:
- matrix: bfloat16 [2, 8, 4, 256, 2, 8, 256], P(None, None, 'prow', None, None, 'pcol'), may hold values from -6 to 6
Outputs:
- image: float32 [2, 8, 4, 256, 2, 8, 256], P(None, None, 'prow', None, None, 'pcol')
All inputs are finite; a program needn't handle non-finite values.
Results may differ from a plain program's by a relative error of at most 0.0003.
Values sent between devices are 32-bit elements; how exact they have to be, the bound alone decides.
A program may use at most 64 MiB of HBM per device.

v0:
```python
import functools

import jax
import jax.numpy as jnp
from jax import lax
from jax.experimental import pallas as pl
from jax.experimental.pallas import tpu as pltpu
from jax.sharding import PartitionSpec as P

F32, BF16 = jnp.float32, jnp.bfloat16
HIGH = lax.Precision.HIGHEST
MESH = pl.DeviceIdType.MESH
NN = (((1,), (0,)), ((), ()))
NT = (((1,), (1,)), ((), ()))


def iotas(rows, cols):
    return (lax.broadcasted_iota(jnp.int32, (rows, cols), 0), lax.broadcasted_iota(jnp.int32, (rows, cols), 1))


def dot(a, b, dims=NN, precision=None):
    return lax.dot_general(a, b, dims, precision=precision, preferred_element_type=F32)


def split3(x):
    hi = x.astype(BF16)
    rest = x - hi.astype(F32)
    mid = rest.astype(BF16)
    return hi, mid, (rest - mid.astype(F32)).astype(BF16)


def carries(np_, nq, rows_here, x_hbm, cum_ref, d_ref, xbuf, rs_loc, cs_loc, t_loc, rs_all, cs_all, t_all,
            in_sem, rs_send, rs_recv, cs_send, cs_recv, t_send, t_recv):
    groups, tile, cols, width = x_hbm.shape
    merged = tile * cols
    p, q = lax.axis_index("prow"), lax.axis_index("pcol")
    total = np_ * nq
    me = p * nq + q
    loads = [pltpu.make_async_copy(x_hbm.at[g], xbuf.at[g], in_sem.at[g]) for g in range(groups)]
    for load in loads:
        load.start()

    barrier = pltpu.get_barrier_semaphore()

    def greet(k, _):
        dev = lax.rem(me + k, total)
        pl.semaphore_signal(barrier, inc=1, device_id=(dev // nq, lax.rem(dev, nq)), device_id_type=MESH)
        return 0

    lax.fori_loop(1, total, greet, 0)

    row_g, _ = iotas(groups, width)
    pick_r, pick_l = iotas(groups * cols, merged)
    rs = jnp.zeros((groups, merged), F32)
    cs = jnp.zeros((groups * cols, width), F32)
    for g in range(groups):
        loads[g].wait()
        x = xbuf[g].reshape(merged, width)
        rs = rs + dot((row_g == g).astype(BF16), x, NT)
        cs = cs + dot((pick_r == g * cols + lax.rem(pick_l, cols)).astype(BF16), x)
    rs_loc[...] = rs
    cs_loc[...] = cs
    t_loc[0] = dot(jnp.ones((8, width), F32), jnp.concatenate(
        [cs, jnp.zeros((128 - groups * cols, width), F32)], axis=0), NT, HIGH)[0:1]
    pl.semaphore_wait(barrier, total - 1)

    def rs_copy(k, sender, target):
        return pltpu.make_async_remote_copy(
            src_ref=rs_loc, dst_ref=rs_all.at[sender], send_sem=rs_send.at[k], recv_sem=rs_recv.at[sender],
            device_id=(p, target), device_id_type=MESH)

    def cs_copy(k, sender, target):
        return pltpu.make_async_remote_copy(
            src_ref=cs_loc, dst_ref=cs_all.at[sender], send_sem=cs_send.at[k], recv_sem=cs_recv.at[sender],
            device_id=(target, q), device_id_type=MESH)

    def t_copy(k, sender, target):
        return pltpu.make_async_remote_copy(
            src_ref=t_loc.at[0], dst_ref=t_all.at[sender], send_sem=t_send.at[k], recv_sem=t_recv.at[sender],
            device_id=(target // nq, lax.rem(target, nq)), device_id_type=MESH)

    kinds = ((t_copy, me, total), (cs_copy, p, np_), (rs_copy, q, nq))
    for make, here, count in kinds:
        def send(k, _):
            make(k, here, lax.rem(here + k, count)).start()
            return 0
        lax.fori_loop(1, count, send, 0)

    def drain(make, here, count):
        def wait(k, _):
            make(k, lax.rem(here + k, count), lax.rem(here + k, count)).wait_recv()
            return 0
        lax.fori_loop(1, count, wait, 0)

    drain(*kinds[0])
    t_all[pl.ds(me, 1)] = t_loc[...]

    def t_sum(k, acc):
        a_all, a_lt, b_all, b_lt = acc
        value = t_all[k]
        kp, kq = k // nq, lax.rem(k, nq)
        left = jnp.where(kq < q, value, 0.0)
        up = jnp.where(kp < p, value, 0.0)
        both = jnp.where(kp < p, left, 0.0)
        return a_all + left, a_lt + both, b_all + value, b_lt + up

    zero = jnp.zeros((1, 128), F32)
    a_all, a_lt, b_all, b_lt = lax.fori_loop(0, total, t_sum, (zero,) * 4)
    out, src = iotas(groups * cols, 128)
    out_g, src_g = out // cols, src // cols
    out_c, src_c = lax.rem(out, cols), lax.rem(src, cols)
    same_g = out_g == src_g
    above = (out_g // rows_here == src_g // rows_here) & (src_g < out_g)

    def pair(strict, equal, all_rows, lt_rows):
        wide = jnp.concatenate([jnp.where(above & strict, 1.0, 0.0), jnp.where(same_g & strict, 1.0, 0.0)], axis=1)
        return jnp.sum(wide * jnp.concatenate([all_rows, lt_rows], axis=1), axis=1, keepdims=True)

    corner = pair(src_c == out_c, None, a_all, a_lt) + pair(src_c < out_c, None, b_all, b_lt)

    drain(*kinds[1])
    c_all, c_lt = cs, jnp.zeros_like(cs)
    for k in range(np_):
        value = jnp.where(k == p, 0.0, cs_all[k])
        c_all = c_all + value
        c_lt = c_lt + jnp.where(k < p, value, 0.0)
    o, s = iotas(groups * cols, groups * cols)
    strict = ((o // (rows_here * cols) == s // (rows_here * cols)) & (lax.rem(o, cols) == lax.rem(s, cols))
              & (s // cols < o // cols)).astype(F32)
    pre = dot(strict, c_all, NN, HIGH) + c_lt
    u0, u1 = iotas(width, width)
    d_ref[...] = dot(pre, (u0 <= u1).astype(F32), NN, HIGH) + corner

    i0, i1 = iotas(merged, merged)
    reach = i1 // cols <= i0 // cols
    c0, c1 = lax.rem(i0, cols), lax.rem(i1, cols)
    low = (reach & (c0 == c1)).astype(BF16)
    low_all = (reach & (c1 < c0)).astype(BF16)
    drain(*kinds[2])
    r_all, r_lt = rs, jnp.zeros_like(rs)
    for k in range(nq):
        value = jnp.where(k == q, 0.0, rs_all[k])
        r_all = r_all + value
        r_lt = r_lt + jnp.where(k < q, value, 0.0)
    cum = jnp.zeros((merged, groups), F32)
    for part_lt, part_all in zip(split3(r_lt), split3(r_all)):
        cum = cum + dot(low, part_lt, NT) + dot(low_all, part_all, NT)
    parts = split3(cum)
    cum_ref[...] = jnp.concatenate(
        [*(part.astype(F32) for part in parts), jnp.zeros((merged, 128 - 3 * groups), F32)], axis=1).astype(BF16)

    for make, here, count in kinds:
        def sent(k, _):
            make(k, here, lax.rem(here + k, count)).wait_send()
            return 0
        lax.fori_loop(1, count, sent, 0)


def finish(np_, nq, rows_here, groups, x_ref, cum_ref, d_ref, o_ref, low_ref, up_ref, cf_ref):
    tile, cols, width = x_ref.shape
    merged = tile * cols
    g = pl.program_id(0)
    p, q = lax.axis_index("prow"), lax.axis_index("pcol")

    @pl.when(g == 0)
    def _():
        i0, i1 = iotas(merged, merged)
        low_ref[...] = ((i1 <= i0) & (lax.rem(i0 - i1 + merged, cols) == 0)).astype(BF16)
        u0, u1 = iotas(width, width)
        up_ref[...] = (u0 <= u1).astype(BF16)
        c0, c1 = iotas(8, width)
        cf_ref[...] = 1.0 / jnp.sqrt((((lax.rem(c0, cols) * nq + q) * width + c1) + 1).astype(F32))

    x = x_ref[...].reshape(merged, width)
    y = dot(low_ref[...], x)
    hi = y.astype(BF16)
    lo = (y - hi.astype(F32)).astype(BF16)
    l0, _ = iotas(128, width)
    pick = ((lax.rem(l0, groups) == g) & (l0 < 3 * groups)).astype(BF16)
    s = dot(hi, up_ref[...]) + dot(lo, up_ref[...]) + dot(cum_ref[...], pick)
    d = d_ref[...].reshape(cols, width)
    dd = jnp.concatenate([d] * (8 // cols), axis=0)
    a0, _ = iotas(merged, 128)
    rf = 1.0 / jnp.sqrt((((lax.rem(g, rows_here) * np_ + p) * tile + a0 // cols) + 1).astype(F32))
    for t in range(width // 128):
        cut = slice(t * 128, (t + 1) * 128)
        part = s[:, cut].reshape(merged // 8, 8, 128) + dd[None, :, cut]
        part = part * (rf.reshape(merged // 8, 8, 128) * cf_ref[:, cut][None])
        o_ref[pl.ds(t, merged, stride=width // 128), :] = part.reshape(merged, 128)


def solution(mesh):
    np_, nq = mesh.shape["prow"], mesh.shape["pcol"]

    def shards(matrix):
        batch, rows_here, _, tile, cols, _, width = matrix.shape
        groups, merged, lanes = batch * rows_here, tile * cols, width // 128
        x = matrix.reshape(groups, tile, cols, width)
        dma = pltpu.SemaphoreType.DMA
        vmem = pl.BlockSpec(memory_space=pltpu.VMEM)
        total = np_ * nq
        cum, d = pl.pallas_call(
            functools.partial(carries, np_, nq, rows_here),
            out_shape=(jax.ShapeDtypeStruct((merged, 128), BF16), jax.ShapeDtypeStruct((groups * cols, width), F32)),
            in_specs=[pl.BlockSpec(memory_space=pl.ANY)],
            out_specs=(vmem, vmem),
            scratch_shapes=[
                pltpu.VMEM((groups, tile, cols, width), BF16),
                pltpu.VMEM((groups, merged), F32),
                pltpu.VMEM((groups * cols, width), F32),
                pltpu.VMEM((1, 1, 128), F32),
                pltpu.VMEM((nq, groups, merged), F32),
                pltpu.VMEM((np_, groups * cols, width), F32),
                pltpu.VMEM((total, 1, 128), F32),
                dma((groups,)), dma((nq,)), dma((nq,)), dma((np_,)), dma((np_,)), dma((total,)), dma((total,)),
            ],
            compiler_params=pltpu.CompilerParams(
                collective_id=0, has_side_effects=True, vmem_limit_bytes=40 * 2**20),
            name="carries",
        )(x)
        out = pl.pallas_call(
            functools.partial(finish, np_, nq, rows_here, groups),
            grid=(groups,),
            out_shape=jax.ShapeDtypeStruct((groups, merged * lanes, 128), F32),
            in_specs=[
                pl.BlockSpec((None, tile, cols, width), lambda g: (g, 0, 0, 0)),
                pl.BlockSpec((merged, 128), lambda g: (0, 0)),
                pl.BlockSpec((None, cols, width), lambda g: (g, 0, 0)),
            ],
            out_specs=pl.BlockSpec((None, merged * lanes, 128), lambda g: (g, 0, 0)),
            scratch_shapes=[pltpu.VMEM((merged, merged), BF16), pltpu.VMEM((width, width), BF16),
                            pltpu.VMEM((8, width), F32)],
            name="finish",
        )(x, cum, d.reshape(groups, cols, width))
        return out.reshape(matrix.shape)

    spec = P(None, None, "prow", None, None, "pcol", None)
    return jax.shard_map(shards, mesh=mesh, in_specs=(spec,), out_specs=spec, check_vma=False)
```

profile of v0, /device:TPU:0, one launch (start us, length us, event | category | flops | bytes accessed | tf_op | source)
XLA Modules:
  0.0 37.9 jit_solution(17615847731895401710)
XLA Ops:
  0.0 0.0 copy-start
  0.0 2.2 %copy-done = bf16[2,8,1,256,2,1,256]{6,4,5,3,2,1,0:T(2,128)(2,1)S(1)} copy-done((bf16[2,8,1,256,2,1,256]{6,4,5,3,2,1,0:T(2,128)(2,1)S(1)}, bf16[2,8,1,256,2,1,256]{6,4,5,3,2,1,0:T(2,128)(2,1)}, u32[]{:S(2)}) %copy-start) | copy-done | bytes 4194328
  2.2 16.7 %carries.1 = (bf16[512,128]{1,0:T(8,128)(2,1)S(1)}, f32[32,256]{1,0:T(8,128)S(1)}) custom-call(bf16[16,256,2,256]{3,2,1,0:T(2,128)(2,1)S(1)} %bitcast.3), custom_call_target="tpu_custom_call" | custom-call | tf_op jit(solution)/shard_map/carries/pallas_call | solution.py:202
  18.9 0.0 copy-start.1
  18.9 0.6 %copy-done.1 = bf16[512,128]{1,0:T(8,128)(2,1)} copy-done((bf16[512,128]{1,0:T(8,128)(2,1)}, bf16[512,128]{1,0:T(8,128)(2,1)S(1)}, u32[]{:S(2)}) %copy-start.1) | copy-done | bytes 131096
  19.6 0.6 %reshape.10.d_ref = f32[16,2,256]{2,1,0:T(2,128)} reshape(f32[32,256]{1,0:T(8,128)S(1)} %get-tuple-element.8) | data formatting | bytes 65536 | tf_op jit(solution)/shard_map/reshape | solution.py:234
  20.2 17.7 %finish.1 = f32[16,1024,128]{2,1,0:T(8,128)} custom-call(bf16[16,256,2,256]{3,2,1,0:T(2,128)(2,1)} %bitcast.2, bf16[512,128]{1,0:T(8,128)(2,1)} %copy-done.1, f32[16,2,256]{2,1,0:T(2,128)} %reshape.10.d_ref), custom_call_target="tpu_custom_call" | custom-call | tf_op jit(solution)/shard_map/finish/pallas_call | solution.py:221
Async XLA Ops:
  0.0 2.2 %copy-start = (bf16[2,8,1,256,2,1,256]{6,4,5,3,2,1,0:T(2,128)(2,1)S(1)}, bf16[2,8,1,256,2,1,256]{6,4,5,3,2,1,0:T(2,128)(2,1)}, u32[]{:S(2)}) copy-start(bf16[2,8,1,256,2,1,256]{6,4,5,3,2,1,0:T(2,128)(2,1)} %param.1) | copy-start | bytes 12582916
  18.9 0.6 %copy-start.1 = (bf16[512,128]{1,0:T(8,128)(2,1)}, bf16[512,128]{1,0:T(8,128)(2,1)S(1)}, u32[]{:S(2)}) copy-start(bf16[512,128]{1,0:T(8,128)(2,1)S(1)} %get-tuple-element.7.cum_ref) | copy-start | bytes 393220
where the time goes:
time: 38.5 us; the launch traced here: 37.9 us
  Pallas kernels  34.5 us (90%)
  local copies, waits for them, and re-layouts  3.46 us (9%)
    pallas_call x1, Pallas kernels, shards(): pl.pallas_call(functools.partial(finish, np_, nq, rows_here, groups), gri...  17.7 us
    pallas_call x1, Pallas kernels, shards(): pl.pallas_call(functools.partial(carries, np_, nq, rows_here), out_shape=...  16.7 us
    unnamed x4, local copies, waits for them, and re-layouts  2.83 us

commit v1 on v0

v1 whole, which is shorter than its diff:
```python
import functools

import jax
import jax.numpy as jnp
from jax import lax
from jax.experimental import pallas as pl
from jax.experimental.pallas import tpu as pltpu
from jax.sharding import PartitionSpec as P

F32, BF16 = jnp.float32, jnp.bfloat16
HIGH = lax.Precision.HIGHEST
MESH = pl.DeviceIdType.MESH
NN = (((1,), (0,)), ((), ()))
SUBS = 8
LANES = 128


def iotas(rows, cols):
    return (lax.broadcasted_iota(jnp.int32, (rows, cols), 0), lax.broadcasted_iota(jnp.int32, (rows, cols), 1))


def local(np_, nq, rows_here, x_hbm, t_ref, c_ref, d_ref, rf_ref, xbuf, up_ref, e_ref, b_ref, k_ref, e_all, b_all, k_all,
          in_sem, e_send, e_recv, b_send, b_recv, k_send, k_recv):
    groups, tile, cols, width = x_hbm.shape
    steps = tile // SUBS
    n = SUBS * cols
    per = LANES // steps
    p, q = lax.axis_index("prow"), lax.axis_index("pcol")
    total = np_ * nq
    me = p * nq + q
    loads = [pltpu.make_async_copy(x_hbm.at[g], xbuf.at[g], in_sem.at[g]) for g in range(groups)]
    for load in loads:
        load.start()

    barrier = pltpu.get_barrier_semaphore()

    def greet(k, _):
        dev = lax.rem(me + k, total)
        pl.semaphore_signal(barrier, inc=1, device_id=(dev // nq, lax.rem(dev, nq)), device_id_type=MESH)
        return 0

    lax.fori_loop(1, total, greet, 0)

    u0, u1 = iotas(width, width)
    up_ref[...] = (u0 <= u1).astype(BF16)
    _, lane = iotas(n, LANES)
    sub, _ = iotas(per * cols, width)

    def block(b, _):
        for k in range(per):
            g = b * per + k
            pltpu.make_async_copy(x_hbm.at[g], xbuf.at[g], in_sem.at[g]).wait()
        e = jnp.zeros((n, LANES), F32)
        bottom = jnp.zeros((per * cols, width), F32)
        for k in range(per):
            g = b * per + k
            x = xbuf[g].reshape(SUBS, steps, cols, width)
            x = jnp.swapaxes(x, 0, 1).reshape(steps * n, width)
            z = lax.dot_general(x, up_ref[...], NN, preferred_element_type=F32)
            acc = jnp.zeros((n, width), F32)
            for i in range(steps):
                acc = acc + z[i * n:(i + 1) * n]
                t_ref[g, pl.ds(i * n, n), :] = acc
                e = jnp.where(lane == k * steps + i, jnp.broadcast_to(acc[:, width - 1:], (n, LANES)), e)
            w = acc[:n // 2] + acc[n // 2:]
            w = w + pltpu.roll(w, cols, 0)
            w = w + pltpu.roll(w, 2 * cols, 0)
            bottom = jnp.where(sub // cols == k, w, bottom)
        e_ref[b] = e
        b_ref[b] = bottom
        return 0

    lax.fori_loop(0, groups // per, block, 0)

    k0, k1 = iotas(per * cols, LANES)
    corner = jnp.zeros((per * cols, LANES), F32)
    for b in range(groups // per):
        edge = jnp.broadcast_to(b_ref[b][:, width - 1:], (per * cols, LANES))
        corner = jnp.where(k1 == b * per * cols + k0, edge, corner)
    k_ref[0] = jnp.sum(corner, axis=0, keepdims=True)
    pl.semaphore_wait(barrier, total - 1)

    def e_copy(k, sender, target):
        return pltpu.make_async_remote_copy(
            src_ref=e_ref, dst_ref=e_all.at[sender], send_sem=e_send.at[k], recv_sem=e_recv.at[sender],
            device_id=(p, target), device_id_type=MESH)

    def b_copy(k, sender, target):
        return pltpu.make_async_remote_copy(
            src_ref=b_ref, dst_ref=b_all.at[sender], send_sem=b_send.at[k], recv_sem=b_recv.at[sender],
            device_id=(target, q), device_id_type=MESH)

    def k_copy(k, sender, target):
        return pltpu.make_async_remote_copy(
            src_ref=k_ref.at[0], dst_ref=k_all.at[sender], send_sem=k_send.at[k], recv_sem=k_recv.at[sender],
            device_id=(target // nq, lax.rem(target, nq)), device_id_type=MESH)

    kinds = ((k_copy, me, total), (b_copy, p, np_), (e_copy, q, nq))
    for make, here, count in kinds:
        def send(k, _):
            make(k, here, lax.rem(here + k, count)).start()
            return 0
        lax.fori_loop(1, count, send, 0)

    def drain(make, here, count):
        def wait(k, _):
            make(k, lax.rem(here + k, count), lax.rem(here + k, count)).wait_recv()
            return 0
        lax.fori_loop(1, count, wait, 0)

    r0, _ = iotas(n, LANES)

    def factors(r, _):
        for i in range(steps):
            row = (r * np_ + p) * tile + (r0 // cols) * steps + i
            rf_ref[r, pl.ds(i * n, n), :] = 1.0 / jnp.sqrt((row + 1).astype(F32))
        return 0

    lax.fori_loop(0, rows_here, factors, 0)

    drain(*kinds[0])
    k_all[pl.ds(me, 1)] = k_ref[...]

    def k_sum(k, acc):
        a_all, a_lt, c_all, c_lt = acc
        value = k_all[k]
        kp, kq = k // nq, lax.rem(k, nq)
        left = jnp.where(kq < q, value, 0.0)
        up = jnp.where(kp < p, value, 0.0)
        both = jnp.where(kp < p, left, 0.0)
        return a_all + left, a_lt + both, c_all + value, c_lt + up

    zero = jnp.zeros((1, LANES), F32)
    a_all, a_lt, c_all, c_lt = lax.fori_loop(0, total, k_sum, (zero,) * 4)
    rows = groups * cols
    out, src = iotas(rows, LANES)
    out_g, src_g = out // cols, src // cols
    out_c, src_c = lax.rem(out, cols), lax.rem(src, cols)
    same_g = out_g == src_g
    above = (out_g // rows_here == src_g // rows_here) & (src_g < out_g)
    weigh = lambda strict, all_rows, lt_rows: (
        jnp.where(above & strict, all_rows, 0.0) + jnp.where(same_g & strict, lt_rows, 0.0))
    corner = jnp.sum(weigh(src_c == out_c, a_all, a_lt) + weigh(src_c < out_c, c_all, c_lt), axis=1, keepdims=True)

    drain(*kinds[1])
    s_all = b_ref[...].reshape(rows, width)
    s_lt = jnp.zeros_like(s_all)
    for k in range(np_):
        value = jnp.where(k == p, 0.0, b_all[k].reshape(rows, width))
        s_all = s_all + value
        s_lt = s_lt + jnp.where(k < p, value, 0.0)
    o, s = iotas(rows, rows)
    strict = ((o // (rows_here * cols) == s // (rows_here * cols)) & (lax.rem(o, cols) == lax.rem(s, cols))
              & (s // cols < o // cols)).astype(F32)
    pre = lax.dot_general(strict, s_all, NN, precision=HIGH, preferred_element_type=F32)
    d_ref[...] = (pre + s_lt + corner).reshape(groups // per, per * cols, width)

    drain(*kinds[2])
    flat = groups // per * n
    r_all = e_ref[...].reshape(flat, LANES)
    r_lt = jnp.zeros_like(r_all)
    for k in range(nq):
        value = jnp.where(k == q, 0.0, e_all[k].reshape(flat, LANES))
        r_all = r_all + value
        r_lt = r_lt + jnp.where(k < q, value, 0.0)
    f0, _ = iotas(flat, LANES)
    for shift in range(1, cols):
        r_lt = r_lt + jnp.where(lax.rem(f0, cols) >= shift, pltpu.roll(r_all, shift, 0), 0.0)
    c_ref[...] = r_lt.reshape(groups // per, n, LANES)

    for make, here, count in kinds:
        def sent(k, _):
            make(k, here, lax.rem(here + k, count)).wait_send()
            return 0
        lax.fori_loop(1, count, sent, 0)


def finish(np_, nq, rows_here, t_ref, c_ref, d_ref, rf_ref, out_hbm, obuf, cb_refs, dp_refs, sem):
    groups, rows, width = t_ref.shape
    cols = out_hbm.shape[3]
    n = SUBS * cols
    steps = rows // n
    per = LANES // steps
    lanes = width // LANES
    q = lax.axis_index("pcol")
    c0, c1 = iotas(n, width)
    cf = 1.0 / jnp.sqrt(((lax.rem(c0, cols) * nq + q) * width + c1 + 1).astype(F32))
    pitch = (steps + 1) * lanes
    sub, _ = iotas(per * cols, width)

    def prepare(g, slot):
        c = pltpu.roll(c_ref[g // per], LANES - lax.rem(g, per) * steps, 1)
        for i in range(steps):
            cb = jnp.broadcast_to(c[:, i:i + 1], (n, LANES))
            cb_refs[slot][pl.ds(i * n, n), :] = cb
        v = t_ref[g, pl.ds((steps - 1) * n, n), :] + jnp.concatenate([cb] * lanes, axis=1)
        v = jnp.where(c0 >= cols, pltpu.roll(v, cols, 0), 0.0)
        shift = cols
        while shift < n:
            v = v + jnp.where(c0 >= shift, pltpu.roll(v, shift, 0), 0.0)
            shift *= 2
        d = jnp.where(sub // cols == lax.rem(g, per), d_ref[g // per], 0.0)
        shift = cols
        while shift < per * cols:
            d = d + pltpu.roll(d, shift, 0)
            shift *= 2
        dp_refs[slot][...] = v + jnp.concatenate([d] * (n // (per * cols)), axis=0)

    def emit(g, slot):
        r = lax.rem(g, rows_here)
        d = dp_refs[slot][...]
        dst = obuf.at[g].reshape(n * (steps + 1) * lanes, LANES)
        for i in range(steps):
            cut = pl.ds(i * n, n)
            cb, v, f = cb_refs[slot][cut, :], t_ref[g, cut, :], rf_ref[r, cut, :]
            for t in range(lanes):
                col = slice(t * LANES, (t + 1) * LANES)
                o = (v[:, col] + (cb + d[:, col])) * (f * cf[:, col])
                for h in range(0, n, 8):
                    dst[pl.ds(h * pitch + i * lanes + t, 8, stride=pitch), :] = o[h:h + 8]

    def copies(g):
        return [pltpu.make_async_copy(obuf.at[g, k, pl.ds(0, steps)], out_hbm.at[g, k // cols, :, k % cols], sem.at[g, k])
                for k in range(n)]

    prepare(0, 0)

    def pair(b, _):
        for slot in range(2):
            g = b * 2 + slot
            prepare(lax.rem(g + 1, groups), 1 - slot)
            emit(g, slot)
            for copy in copies(g):
                copy.start()
        return 0

    lax.fori_loop(0, groups // 2, pair, 0)

    def drain(g, _):
        for copy in copies(g):
            copy.wait()
        return 0

    lax.fori_loop(0, groups, drain, 0)


def solution(mesh):
    np_, nq = mesh.shape["prow"], mesh.shape["pcol"]

    def shards(matrix):
        batch, rows_here, _, tile, cols, _, width = matrix.shape
        groups, lanes = batch * rows_here, width // LANES
        steps, n, total = tile // SUBS, SUBS * cols, np_ * nq
        per = LANES // steps
        blocks = groups // per
        x = pltpu.with_memory_space_constraint(matrix.reshape(groups, tile, cols, width), pltpu.HBM)
        dma = pltpu.SemaphoreType.DMA
        vmem = pl.BlockSpec(memory_space=pltpu.VMEM)
        carried = pl.pallas_call(
            functools.partial(local, np_, nq, rows_here),
            out_shape=(jax.ShapeDtypeStruct((groups, tile * cols, width), F32),
                       jax.ShapeDtypeStruct((blocks, n, LANES), F32),
                       jax.ShapeDtypeStruct((blocks, per * cols, width), F32),
                       jax.ShapeDtypeStruct((rows_here, tile * cols, LANES), F32)),
            in_specs=[pl.BlockSpec(memory_space=pltpu.HBM)],
            out_specs=(vmem,) * 4,
            scratch_shapes=[
                pltpu.VMEM((groups, tile, cols, width), BF16),
                pltpu.VMEM((width, width), BF16),
                pltpu.VMEM((blocks, n, LANES), F32),
                pltpu.VMEM((blocks, per * cols, width), F32),
                pltpu.VMEM((1, 1, LANES), F32),
                pltpu.VMEM((nq, blocks, n, LANES), F32),
                pltpu.VMEM((np_, blocks, per * cols, width), F32),
                pltpu.VMEM((total, 1, LANES), F32),
                dma((groups,)), dma((nq,)), dma((nq,)), dma((np_,)), dma((np_,)), dma((total,)), dma((total,)),
            ],
            compiler_params=pltpu.CompilerParams(
                collective_id=0, has_side_effects=True, vmem_limit_bytes=24 * 2**20),
            name="local",
        )(x)
        out = pl.pallas_call(
            functools.partial(finish, np_, nq, rows_here),
            out_shape=jax.ShapeDtypeStruct((groups, SUBS, steps, cols, lanes, LANES), F32),
            in_specs=[vmem] * 4,
            out_specs=pl.BlockSpec(memory_space=pl.ANY),
            scratch_shapes=[
                pltpu.VMEM((groups, n, steps + 1, lanes, LANES), F32),
                [pltpu.VMEM((tile * cols, LANES), F32)] * 2,
                [pltpu.VMEM((n, width), F32)] * 2,
                dma((groups, n)),
            ],
            compiler_params=pltpu.CompilerParams(vmem_limit_bytes=24 * 2**20),
            name="finish",
        )(*carried)
        return out.reshape(matrix.shape)

    spec = P(None, None, "prow", None, None, "pcol", None)
    return jax.shard_map(shards, mesh=mesh, in_specs=(spec,), out_specs=spec, check_vma=False)
```

time: 38.5 us -> 23.8 us (0.62); the launches traced: 37.9 us -> 23.7 us
  Pallas kernels: 34.5 us -> 23.7 us
  local copies, waits for them, and re-layouts: 3.46 us -> 0 us
    pallas_call x2, Pallas kernels: 34.5 us -> 23.7 us  [the longest x1 15.7 us: shards(): pl.pallas_call(functools.partial(local, np_, nq, rows_here), out_shape=(j...]
    unnamed x4 -> x0, local copies, waits for them, and re-layouts: 2.83 us -> none
    reshape x1 -> x0, local copies, waits for them, and re-layouts: 0.64 us -> none  [shards(): d.reshape(groups, cols, width)]
where the time goes in v1:
time: 23.8 us; the launch traced here: 23.7 us
  Pallas kernels  23.7 us (100%)
    pallas_call x1, Pallas kernels, shards(): pl.pallas_call(functools.partial(local, np_, nq, rows_here), out_shape=(j...  15.7 us
    pallas_call x1, Pallas kernels, shards(): pl.pallas_call(functools.partial(finish, np_, nq, rows_here), out_shape=j...  7.98 us

profile of v1, /device:TPU:0, one launch (start us, length us, event | category | flops | bytes accessed | tf_op | source)
XLA Modules:
  0.0 23.7 jit_solution(2998143538896276152)
XLA Ops:
  0.0 15.7 %local.1 = (f32[16,512,256]{2,1,0:T(8,128)S(1)}, f32[4,16,128]{2,1,0:T(8,128)S(1)}, f32[4,8,256]{2,1,0:T(8,128)S(1)}, f32[8,512,128]{2,1,0:T(8,128)S(1)}) custom-call(bf16[16,256,2,256]{3,2,1,0:T(2,128)(2,1)} %bitcast.2), custom_call_target="tpu_custom_call" | custom-call | tf_op jit(solution)/shard_map/local/pallas_call | solution.py:259
  15.7 8.0 %finish.1 = f32[16,8,32,2,2,128]{5,4,3,2,1,0:T(2,128)} custom-call(f32[16,512,256]{2,1,0:T(8,128)S(1)} %get-tuple-element.9.t_ref, f32[4,16,128]{2,1,0:T(8,128)S(1)} %get-tuple-element.10.c_ref, f32[4,8,256]{2,1,0:T(8,128)S(1)} %get-tuple-element.11.d_ref, f32[8,512,128]{2,1,0:T(8,128)S(1)} %get-tuple-element.12.rf_ref), custom_call_target="tpu_custom_call" | custom-call | tf_op jit(solution)/shard_map/finish/pallas_call | solution.py:282

commit v2 on v1

--- a/solution.py
+++ b/solution.py
@@ -19,7 +19,16 @@
     return (lax.broadcasted_iota(jnp.int32, (rows, cols), 0), lax.broadcasted_iota(jnp.int32, (rows, cols), 1))
 
 
-def local(np_, nq, rows_here, x_hbm, t_ref, c_ref, d_ref, rf_ref, xbuf, up_ref, e_ref, b_ref, k_ref, e_all, b_all, k_all,
+def shifted(v, rows, cols, count):
+    v = jnp.where(rows >= cols, pltpu.roll(v, cols, 0), 0.0)
+    shift = cols
+    while shift < count:
+        v = v + jnp.where(rows >= shift, pltpu.roll(v, shift, 0), 0.0)
+        shift *= 2
+    return v
+
+
+def local(np_, nq, rows_here, x_hbm, t_ref, pt_ref, c_ref, d_ref, rf_ref, xbuf, up_ref, e_ref, b_ref, k_ref, e_all, b_all, k_all,
           in_sem, e_send, e_recv, b_send, b_recv, k_send, k_recv):
     groups, tile, cols, width = x_hbm.shape
     steps = tile // SUBS
@@ -43,7 +52,8 @@
 
     u0, u1 = iotas(width, width)
     up_ref[...] = (u0 <= u1).astype(BF16)
-    _, lane = iotas(n, LANES)
+    s0, lane = iotas(n, LANES)
+    w0, _ = iotas(n, width)
     sub, _ = iotas(per * cols, width)
 
     def block(b, _):
@@ -62,10 +72,15 @@
                 acc = acc + z[i * n:(i + 1) * n]
                 t_ref[g, pl.ds(i * n, n), :] = acc
                 e = jnp.where(lane == k * steps + i, jnp.broadcast_to(acc[:, width - 1:], (n, LANES)), e)
+            pt_ref[g] = shifted(acc, w0, cols, n)
             w = acc[:n // 2] + acc[n // 2:]
             w = w + pltpu.roll(w, cols, 0)
             w = w + pltpu.roll(w, 2 * cols, 0)
             bottom = jnp.where(sub // cols == k, w, bottom)
+        down = shifted(e, s0, cols, n)
+        for k in range(per):
+            last = jnp.broadcast_to(down[:, (k + 1) * steps - 1:(k + 1) * steps], (n, LANES))
+            e = e + jnp.where(lane // steps == k, last, 0.0)
         e_ref[b] = e
         b_ref[b] = bottom
         return 0
@@ -175,7 +190,7 @@
         lax.fori_loop(1, count, sent, 0)
 
 
-def finish(np_, nq, rows_here, t_ref, c_ref, d_ref, rf_ref, out_hbm, obuf, cb_refs, dp_refs, sem):
+def finish(np_, nq, rows_here, t_ref, pt_ref, c_ref, d_ref, rf_ref, out_hbm, obuf, cb_refs, sem):
     groups, rows, width = t_ref.shape
     cols = out_hbm.shape[3]
     n = SUBS * cols
@@ -188,57 +203,51 @@
     pitch = (steps + 1) * lanes
     sub, _ = iotas(per * cols, width)
 
-    def prepare(g, slot):
-        c = pltpu.roll(c_ref[g // per], LANES - lax.rem(g, per) * steps, 1)
-        for i in range(steps):
-            cb = jnp.broadcast_to(c[:, i:i + 1], (n, LANES))
-            cb_refs[slot][pl.ds(i * n, n), :] = cb
-        v = t_ref[g, pl.ds((steps - 1) * n, n), :] + jnp.concatenate([cb] * lanes, axis=1)
-        v = jnp.where(c0 >= cols, pltpu.roll(v, cols, 0), 0.0)
-        shift = cols
-        while shift < n:
-            v = v + jnp.where(c0 >= shift, pltpu.roll(v, shift, 0), 0.0)
-            shift *= 2
-        d = jnp.where(sub // cols == lax.rem(g, per), d_ref[g // per], 0.0)
-        shift = cols
-        while shift < per * cols:
-            d = d + pltpu.roll(d, shift, 0)
-            shift *= 2
-        dp_refs[slot][...] = v + jnp.concatenate([d] * (n // (per * cols)), axis=0)
-
-    def emit(g, slot):
-        r = lax.rem(g, rows_here)
-        d = dp_refs[slot][...]
-        dst = obuf.at[g].reshape(n * (steps + 1) * lanes, LANES)
-        for i in range(steps):
-            cut = pl.ds(i * n, n)
-            cb, v, f = cb_refs[slot][cut, :], t_ref[g, cut, :], rf_ref[r, cut, :]
-            for t in range(lanes):
-                col = slice(t * LANES, (t + 1) * LANES)
-                o = (v[:, col] + (cb + d[:, col])) * (f * cf[:, col])
-                for h in range(0, n, 8):
-                    dst[pl.ds(h * pitch + i * lanes + t, 8, stride=pitch), :] = o[h:h + 8]
-
     def copies(g):
-        return [pltpu.make_async_copy(obuf.at[g, k, pl.ds(0, steps)], out_hbm.at[g, k // cols, :, k % cols], sem.at[g, k])
+        return [pltpu.make_async_copy(obuf.at[g, k, pl.ds(0, steps)], out_hbm.at[g, k // cols, :, k % cols], sem.at[g])
                 for k in range(n)]
 
-    prepare(0, 0)
-
-    def pair(b, _):
+    def turned(g):
+        return pltpu.roll(c_ref[g // per], LANES - lax.rem(g, per) * steps, 1)
+
+    def spread(c, i):
+        return jnp.broadcast_to(c[:, i:i + 1], (n, LANES))
+
+    first = turned(0)
+    for i in range(steps):
+        cb_refs[0][pl.ds(i * n, n), :] = spread(first, i)
+
+    def pair(b, ahead):
         for slot in range(2):
             g = b * 2 + slot
-            prepare(lax.rem(g + 1, groups), 1 - slot)
-            emit(g, slot)
+            r = lax.rem(g, rows_here)
+            d = jnp.where(sub // cols == lax.rem(g, per), d_ref[g // per], 0.0)
+            shift = cols
+            while shift < per * cols:
+                d = d + pltpu.roll(d, shift, 0)
+                shift *= 2
+            d = pt_ref[g] + jnp.concatenate([d] * (n // (per * cols)), axis=0)
+            dst = obuf.at[g].reshape(n * pitch, LANES)
+            later = turned(lax.rem(g + 2, groups))
+            for i in range(steps):
+                cb_refs[1 - slot][pl.ds(i * n, n), :] = spread(ahead, i)
+            for i in range(steps):
+                cut = pl.ds(i * n, n)
+                cb, v, f = cb_refs[slot][cut, :], t_ref[g, cut, :], rf_ref[r, cut, :]
+                for t in range(lanes):
+                    col = slice(t * LANES, (t + 1) * LANES)
+                    o = (v[:, col] + (cb + d[:, col])) * (f * cf[:, col])
+                    for h in range(0, n, 8):
+                        dst[pl.ds(h * pitch + i * lanes + t, 8, stride=pitch), :] = o[h:h + 8]
+            ahead = later
             for copy in copies(g):
                 copy.start()
-        return 0
-
-    lax.fori_loop(0, groups // 2, pair, 0)
+        return ahead
+
+    lax.fori_loop(0, groups // 2, pair, turned(1))
 
     def drain(g, _):
-        for copy in copies(g):
-            copy.wait()
+        pltpu.make_async_copy(out_hbm.at[g], out_hbm.at[g], sem.at[g]).wait()
         return 0
 
     lax.fori_loop(0, groups, drain, 0)
@@ -259,11 +268,12 @@
         carried = pl.pallas_call(
             functools.partial(local, np_, nq, rows_here),
             out_shape=(jax.ShapeDtypeStruct((groups, tile * cols, width), F32),
+                       jax.ShapeDtypeStruct((groups, n, width), F32),
                        jax.ShapeDtypeStruct((blocks, n, LANES), F32),
                        jax.ShapeDtypeStruct((blocks, per * cols, width), F32),
                        jax.ShapeDtypeStruct((rows_here, tile * cols, LANES), F32)),
             in_specs=[pl.BlockSpec(memory_space=pltpu.HBM)],
-            out_specs=(vmem,) * 4,
+            out_specs=(vmem,) * 5,
             scratch_shapes=[
                 pltpu.VMEM((groups, tile, cols, width), BF16),
                 pltpu.VMEM((width, width), BF16),
@@ -282,13 +292,12 @@
         out = pl.pallas_call(
             functools.partial(finish, np_, nq, rows_here),
             out_shape=jax.ShapeDtypeStruct((groups, SUBS, steps, cols, lanes, LANES), F32),
-            in_specs=[vmem] * 4,
+            in_specs=[vmem] * 5,
             out_specs=pl.BlockSpec(memory_space=pl.ANY),
             scratch_shapes=[
                 pltpu.VMEM((groups, n, steps + 1, lanes, LANES), F32),
                 [pltpu.VMEM((tile * cols, LANES), F32)] * 2,
-                [pltpu.VMEM((n, width), F32)] * 2,
-                dma((groups, n)),
+                dma((groups,)),
             ],
             compiler_params=pltpu.CompilerParams(vmem_limit_bytes=24 * 2**20),
             name="finish",

time: 23.8 us -> 19.8 us (0.83)
  Pallas kernels: 23.7 us -> 19.6 us
    pallas_call x1, Pallas kernels: 7.98 us -> 3.57 us  [shards(): pl.pallas_call(functools.partial(finish, np_, nq, rows_here), out_shape=j...]
    pallas_call x1, Pallas kernels: 15.7 us -> 16.1 us  [shards(): pl.pallas_call(functools.partial(local, np_, nq, rows_here), out_shape=(j...]
where the time goes in v2:
time: 19.8 us; the launch traced here: 19.6 us
  Pallas kernels  19.6 us (99%)
    pallas_call x1, Pallas kernels, shards(): pl.pallas_call(functools.partial(local, np_, nq, rows_here), out_shape=(j...  16.1 us
    pallas_call x1, Pallas kernels, shards(): pl.pallas_call(functools.partial(finish, np_, nq, rows_here), out_shape=j...  3.57 us

profile of v2, /device:TPU:0, one launch (start us, length us, event | category | flops | bytes accessed | tf_op | source)
XLA Modules:
  0.0 19.6 jit_solution(3149074453077167333)
XLA Ops:
  0.0 16.1 %local.1 = (f32[16,512,256]{2,1,0:T(8,128)S(1)}, f32[16,16,256]{2,1,0:T(8,128)S(1)}, f32[4,16,128]{2,1,0:T(8,128)S(1)}, f32[4,8,256]{2,1,0:T(8,128)S(1)}, f32[8,512,128]{2,1,0:T(8,128)S(1)}) custom-call(bf16[16,256,2,256]{3,2,1,0:T(2,128)(2,1)} %bitcast.2), custom_call_target="tpu_custom_call" | custom-call | tf_op jit(solution)/shard_map/local/pallas_call | solution.py:268
  16.1 3.6 %finish.1 = f32[16,8,32,2,2,128]{5,4,3,2,1,0:T(2,128)} custom-call(f32[16,512,256]{2,1,0:T(8,128)S(1)} %get-tuple-element.10.t_ref, f32[16,16,256]{2,1,0:T(8,128)S(1)} %get-tuple-element.11.pt_ref, f32[4,16,128]{2,1,0:T(8,128)S(1)} %get-tuple-element.12.c_ref, f32[4,8,256]{2,1,0:T(8,128)S(1)} %get-tuple-element.13.d_ref, ...), custom_call_target="tpu_custom_call" | custom-call | tf_op jit(solution)/shard_map/finish/pallas_call | solution.py:292

commit v3 on v2

--- a/solution.py
+++ b/solution.py
@@ -13,6 +13,7 @@
 NN = (((1,), (0,)), ((), ()))
 SUBS = 8
 LANES = 128
+CHUNKS = 2
 
 
 def iotas(rows, cols):
@@ -28,12 +29,14 @@
     return v
 
 
-def local(np_, nq, rows_here, x_hbm, t_ref, pt_ref, c_ref, d_ref, rf_ref, xbuf, up_ref, e_ref, b_ref, k_ref, e_all, b_all, k_all,
-          in_sem, e_send, e_recv, b_send, b_recv, k_send, k_recv):
+def local(np_, nq, rows_here, x_hbm, t_ref, pt_ref, c_ref, d_ref, rf_ref, xbuf, up_ref, e_tmp, e_ref, b_ref, k_ref,
+          e_all, b_all, k_all, in_sem, e_send, e_recv, f_send, f_recv, b_send, b_recv, k_send, k_recv):
     groups, tile, cols, width = x_hbm.shape
     steps = tile // SUBS
     n = SUBS * cols
     per = LANES // steps
+    blocks = groups // per
+    chunks, _, part = e_ref.shape[:3]
     p, q = lax.axis_index("prow"), lax.axis_index("pcol")
     total = np_ * nq
     me = p * nq + q
@@ -41,14 +44,22 @@
     for load in loads:
         load.start()
 
+    def around(i, j):
+        return lax.rem(p + i, np_), lax.rem(q + j, nq)
+
+    def others(visit):
+        for j in range(1, nq):
+            visit(p, lax.rem(q + j, nq), j)
+
+        def row(i, _):
+            for j in range(nq):
+                visit(*around(i, j), i * nq + j)
+            return 0
+
+        lax.fori_loop(1, np_, row, 0)
+
     barrier = pltpu.get_barrier_semaphore()
-
-    def greet(k, _):
-        dev = lax.rem(me + k, total)
-        pl.semaphore_signal(barrier, inc=1, device_id=(dev // nq, lax.rem(dev, nq)), device_id_type=MESH)
-        return 0
-
-    lax.fori_loop(1, total, greet, 0)
+    others(lambda tp, tq, k: pl.semaphore_signal(barrier, inc=1, device_id=(tp, tq), device_id_type=MESH))
 
     u0, u1 = iotas(width, width)
     up_ref[...] = (u0 <= u1).astype(BF16)
@@ -56,7 +67,7 @@
     w0, _ = iotas(n, width)
     sub, _ = iotas(per * cols, width)
 
-    def block(b, _):
+    def block(b, h):
         for k in range(per):
             g = b * per + k
             pltpu.make_async_copy(x_hbm.at[g], xbuf.at[g], in_sem.at[g]).wait()
@@ -81,47 +92,65 @@
         for k in range(per):
             last = jnp.broadcast_to(down[:, (k + 1) * steps - 1:(k + 1) * steps], (n, LANES))
             e = e + jnp.where(lane // steps == k, last, 0.0)
-        e_ref[b] = e
+        e_tmp[...] = e
+        for c in range(cols):
+            e_ref[h, c, b - h * part] = e_tmp[pl.ds(c, SUBS, stride=cols), :]
         b_ref[b] = bottom
-        return 0
-
-    lax.fori_loop(0, groups // per, block, 0)
-
-    k0, k1 = iotas(per * cols, LANES)
-    corner = jnp.zeros((per * cols, LANES), F32)
-    for b in range(groups // per):
-        edge = jnp.broadcast_to(b_ref[b][:, width - 1:], (per * cols, LANES))
-        corner = jnp.where(k1 == b * per * cols + k0, edge, corner)
-    k_ref[0] = jnp.sum(corner, axis=0, keepdims=True)
-    pl.semaphore_wait(barrier, total - 1)
-
-    def e_copy(k, sender, target):
+        return h
+
+    def most(h, k, sender, target):
         return pltpu.make_async_remote_copy(
-            src_ref=e_ref, dst_ref=e_all.at[sender], send_sem=e_send.at[k], recv_sem=e_recv.at[sender],
-            device_id=(p, target), device_id_type=MESH)
+            src_ref=e_ref.at[h, pl.ds(0, cols - 1)], dst_ref=e_all.at[sender, h, pl.ds(0, cols - 1)],
+            send_sem=e_send.at[h, k], recv_sem=e_recv.at[h, sender], device_id=(p, target), device_id_type=MESH)
+
+    def last(h, k, sender, target):
+        return pltpu.make_async_remote_copy(
+            src_ref=e_ref.at[h, cols - 1], dst_ref=e_all.at[sender, h, cols - 1],
+            send_sem=f_send.at[h, k], recv_sem=f_recv.at[h, sender], device_id=(p, target), device_id_type=MESH)
 
     def b_copy(k, sender, target):
         return pltpu.make_async_remote_copy(
             src_ref=b_ref, dst_ref=b_all.at[sender], send_sem=b_send.at[k], recv_sem=b_recv.at[sender],
             device_id=(target, q), device_id_type=MESH)
 
-    def k_copy(k, sender, target):
+    def k_copy(tp, tq, k):
         return pltpu.make_async_remote_copy(
-            src_ref=k_ref.at[0], dst_ref=k_all.at[sender], send_sem=k_send.at[k], recv_sem=k_recv.at[sender],
-            device_id=(target // nq, lax.rem(target, nq)), device_id_type=MESH)
-
-    kinds = ((k_copy, me, total), (b_copy, p, np_), (e_copy, q, nq))
-    for make, here, count in kinds:
-        def send(k, _):
-            make(k, here, lax.rem(here + k, count)).start()
-            return 0
-        lax.fori_loop(1, count, send, 0)
-
-    def drain(make, here, count):
-        def wait(k, _):
-            make(k, lax.rem(here + k, count), lax.rem(here + k, count)).wait_recv()
-            return 0
-        lax.fori_loop(1, count, wait, 0)
+            src_ref=k_ref.at[0], dst_ref=k_all.at[me], send_sem=k_send.at[k], recv_sem=k_recv,
+            device_id=(tp, tq), device_id_type=MESH)
+
+    def send_edges(h):
+        for k in range(1, nq):
+            target = lax.rem(q + k, nq)
+            most(h, k, q, target).start()
+
+            @pl.when(target > q)
+            def _():
+                last(h, k, q, target).start()
+
+    late = 4 * q >= 3 * nq
+
+    def meet():
+        pl.semaphore_wait(barrier, total - 1)
+        for h in range(chunks - 1):
+            send_edges(h)
+
+    for h in range(chunks):
+        if h == chunks - 1:
+            pl.when(late)(meet)
+        lax.fori_loop(h * part, (h + 1) * part, block, h)
+    pl.when(jnp.logical_not(late))(meet)
+
+    k0, k1 = iotas(per * cols, LANES)
+    corner = jnp.zeros((per * cols, LANES), F32)
+    for b in range(blocks):
+        edge = jnp.broadcast_to(b_ref[b][:, width - 1:], (per * cols, LANES))
+        corner = jnp.where(k1 == b * per * cols + k0, edge, corner)
+    k_ref[0] = jnp.sum(corner, axis=0, keepdims=True)
+    k_all[pl.ds(me, 1)] = k_ref[...]
+    others(lambda tp, tq, k: k_copy(tp, tq, k).start())
+    send_edges(chunks - 1)
+    for k in range(1, np_):
+        b_copy(k, p, lax.rem(p + k, np_)).start()
 
     r0, _ = iotas(n, LANES)
 
@@ -133,31 +162,10 @@
 
     lax.fori_loop(0, rows_here, factors, 0)
 
-    drain(*kinds[0])
-    k_all[pl.ds(me, 1)] = k_ref[...]
-
-    def k_sum(k, acc):
-        a_all, a_lt, c_all, c_lt = acc
-        value = k_all[k]
-        kp, kq = k // nq, lax.rem(k, nq)
-        left = jnp.where(kq < q, value, 0.0)
-        up = jnp.where(kp < p, value, 0.0)
-        both = jnp.where(kp < p, left, 0.0)
-        return a_all + left, a_lt + both, c_all + value, c_lt + up
-
-    zero = jnp.zeros((1, LANES), F32)
-    a_all, a_lt, c_all, c_lt = lax.fori_loop(0, total, k_sum, (zero,) * 4)
+    for k in range(1, np_):
+        sender = lax.rem(p + k, np_)
+        b_copy(k, sender, sender).wait_recv()
     rows = groups * cols
-    out, src = iotas(rows, LANES)
-    out_g, src_g = out // cols, src // cols
-    out_c, src_c = lax.rem(out, cols), lax.rem(src, cols)
-    same_g = out_g == src_g
-    above = (out_g // rows_here == src_g // rows_here) & (src_g < out_g)
-    weigh = lambda strict, all_rows, lt_rows: (
-        jnp.where(above & strict, all_rows, 0.0) + jnp.where(same_g & strict, lt_rows, 0.0))
-    corner = jnp.sum(weigh(src_c == out_c, a_all, a_lt) + weigh(src_c < out_c, c_all, c_lt), axis=1, keepdims=True)
-
-    drain(*kinds[1])
     s_all = b_ref[...].reshape(rows, width)
     s_lt = jnp.zeros_like(s_all)
     for k in range(np_):
@@ -168,26 +176,57 @@
     strict = ((o // (rows_here * cols) == s // (rows_here * cols)) & (lax.rem(o, cols) == lax.rem(s, cols))
               & (s // cols < o // cols)).astype(F32)
     pre = lax.dot_general(strict, s_all, NN, precision=HIGH, preferred_element_type=F32)
-    d_ref[...] = (pre + s_lt + corner).reshape(groups // per, per * cols, width)
-
-    drain(*kinds[2])
-    flat = groups // per * n
-    r_all = e_ref[...].reshape(flat, LANES)
-    r_lt = jnp.zeros_like(r_all)
-    for k in range(nq):
-        value = jnp.where(k == q, 0.0, e_all[k].reshape(flat, LANES))
-        r_all = r_all + value
-        r_lt = r_lt + jnp.where(k < q, value, 0.0)
-    f0, _ = iotas(flat, LANES)
-    for shift in range(1, cols):
-        r_lt = r_lt + jnp.where(lax.rem(f0, cols) >= shift, pltpu.roll(r_all, shift, 0), 0.0)
-    c_ref[...] = r_lt.reshape(groups // per, n, LANES)
-
-    for make, here, count in kinds:
-        def sent(k, _):
-            make(k, here, lax.rem(here + k, count)).wait_send()
-            return 0
-        lax.fori_loop(1, count, sent, 0)
+    d_ref[...] = (pre + s_lt).reshape(blocks, per * cols, width)
+
+    for h in range(chunks):
+        for k in range(1, nq):
+            sender = lax.rem(q + k, nq)
+            most(h, k, sender, sender).wait_recv()
+
+            @pl.when(sender < q)
+            def _():
+                last(h, k, sender, sender).wait_recv()
+
+        base = jnp.zeros((part, SUBS, LANES), F32)
+        for c in range(cols):
+            whole, before = e_ref[h, c], jnp.zeros((part, SUBS, LANES), F32)
+            for k in range(nq):
+                value = e_all[k, h, c]
+                before = before + jnp.where(k < q, value, 0.0)
+                if c < cols - 1:
+                    whole = whole + jnp.where(k == q, 0.0, value)
+            for b in range(part):
+                c_ref[h * part + b, pl.ds(c, SUBS, stride=cols), :] = (base + before)[b]
+            base = base + whole
+
+    others(lambda tp, tq, k: k_copy(tp, tq, k).wait_send())
+    for k in range(1, np_):
+        b_copy(k, p, p).wait_send()
+    for h in range(chunks):
+        for k in range(1, nq):
+            target = lax.rem(q + k, nq)
+            most(h, k, q, target).wait_send()
+
+            @pl.when(target > q)
+            def _():
+                last(h, k, q, target).wait_send()
+
+    pltpu.make_async_copy(k_all.at[pl.ds(0, total - 1)], k_all.at[pl.ds(0, total - 1)], k_recv).wait()
+    value = k_all.reshape(total, LANES)[...]
+    d0, _ = iotas(total, LANES)
+    left = jnp.where(lax.rem(d0, nq) < q, value, 0.0)
+    add = lambda v: jnp.sum(v, axis=0, keepdims=True)
+    a_all, a_lt = add(left), add(jnp.where(d0 // nq < p, left, 0.0))
+    c_all, c_lt = add(value), add(jnp.where(d0 // nq < p, value, 0.0))
+    out, src = iotas(rows, LANES)
+    out_g, src_g = out // cols, src // cols
+    out_c, src_c = lax.rem(out, cols), lax.rem(src, cols)
+    same_g = out_g == src_g
+    above = (out_g // rows_here == src_g // rows_here) & (src_g < out_g)
+    weigh = lambda strict, all_rows, lt_rows: (
+        jnp.where(above & strict, all_rows, 0.0) + jnp.where(same_g & strict, lt_rows, 0.0))
+    corner = jnp.sum(weigh(src_c == out_c, a_all, a_lt) + weigh(src_c < out_c, c_all, c_lt), axis=1, keepdims=True)
+    d_ref[...] = d_ref[...] + corner.reshape(blocks, per * cols, 1)
 
 
 def finish(np_, nq, rows_here, t_ref, pt_ref, c_ref, d_ref, rf_ref, out_hbm, obuf, cb_refs, sem):
@@ -277,13 +316,15 @@
             scratch_shapes=[
                 pltpu.VMEM((groups, tile, cols, width), BF16),
                 pltpu.VMEM((width, width), BF16),
-                pltpu.VMEM((blocks, n, LANES), F32),
+                pltpu.VMEM((n, LANES), F32),
+                pltpu.VMEM((CHUNKS, cols, blocks // CHUNKS, SUBS, LANES), F32),
                 pltpu.VMEM((blocks, per * cols, width), F32),
                 pltpu.VMEM((1, 1, LANES), F32),
-                pltpu.VMEM((nq, blocks, n, LANES), F32),
+                pltpu.VMEM((nq, CHUNKS, cols, blocks // CHUNKS, SUBS, LANES), F32),
                 pltpu.VMEM((np_, blocks, per * cols, width), F32),
                 pltpu.VMEM((total, 1, LANES), F32),
-                dma((groups,)), dma((nq,)), dma((nq,)), dma((np_,)), dma((np_,)), dma((total,)), dma((total,)),
+                dma((groups,)), dma((CHUNKS, nq)), dma((CHUNKS, nq)), dma((CHUNKS, nq)), dma((CHUNKS, nq)),
+                dma((np_,)), dma((np_,)), dma((total,)), dma,
             ],
             compiler_params=pltpu.CompilerParams(
                 collective_id=0, has_side_effects=True, vmem_limit_bytes=24 * 2**20),

time: 19.8 us -> 17.9 us (0.904)
  Pallas kernels: 19.6 us -> 17.8 us
    pallas_call x1, Pallas kernels: 16.1 us -> 14.2 us  [shards(): pl.pallas_call(functools.partial(local, np_, nq, rows_here), out_shape=(j...]
where the time goes in v3:
time: 17.9 us; the launch traced here: 17.8 us
  Pallas kernels  17.8 us (99%)
    pallas_call x1, Pallas kernels, shards(): pl.pallas_call(functools.partial(local, np_, nq, rows_here), out_shape=(j...  14.2 us
    pallas_call x1, Pallas kernels, shards(): pl.pallas_call(functools.partial(finish, np_, nq, rows_here), out_shape=j...  3.57 us

profile of v3, /device:TPU:0, one launch (start us, length us, event | category | flops | bytes accessed | tf_op | source)
XLA Modules:
  0.0 17.8 jit_solution(9434432891173663116)
XLA Ops:
  0.0 14.2 %local.1 = (f32[16,512,256]{2,1,0:T(8,128)S(1)}, f32[16,16,256]{2,1,0:T(8,128)S(1)}, f32[4,16,128]{2,1,0:T(8,128)S(1)}, f32[4,8,256]{2,1,0:T(8,128)S(1)}, f32[8,512,128]{2,1,0:T(8,128)S(1)}) custom-call(bf16[16,256,2,256]{3,2,1,0:T(2,128)(2,1)} %bitcast.2), custom_call_target="tpu_custom_call" | custom-call | tf_op jit(solution)/shard_map/local/pallas_call | solution.py:307
  14.2 3.6 %finish.1 = f32[16,8,32,2,2,128]{5,4,3,2,1,0:T(2,128)} custom-call(f32[16,512,256]{2,1,0:T(8,128)S(1)} %get-tuple-element.10.t_ref, f32[16,16,256]{2,1,0:T(8,128)S(1)} %get-tuple-element.11.pt_ref, f32[4,16,128]{2,1,0:T(8,128)S(1)} %get-tuple-element.12.c_ref, f32[4,8,256]{2,1,0:T(8,128)S(1)} %get-tuple-element.13.d_ref, ...), custom_call_target="tpu_custom_call" | custom-call | tf_op jit(solution)/shard_map/finish/pallas_call | solution.py:333
